TPU v7x, 32 devices: a whole 2x2x4 slice. The times are simulated.
32 devices in a mesh: date: 8 (over z, x), pix: 4 (over y, core).
Axes of the slice: x: 2, y: 2, z: 4, core: 2. Of those that a mesh axis runs over, the one named last changes fastest.
Arguments:
- stack: bfloat16 [8, 10, 32, 2048], P('date', None, 'pix'), may hold values from -4 to 12
- cloud: int32 [8, 32, 2048], P('date', 'pix'), may hold values 0 or 1
Outputs:
- composite: float32 [10, 32, 2048], P(None, 'pix')
All inputs are finite; a program needn't handle non-finite values. No bound on the sum of `cloud` on one device may be relied on, other than what follows from the above.
Results may differ from a plain program's by a relative error of at most 0.0003.
Values may be sent and summed in bfloat16 or wider, within the bound.
No kernel may reach another device: no remote copies, remote signals or barrier semaphores. Data moves between devices by JAX's collectives and lax.ppermute only.
A program may use at most 64 MiB of HBM per device.

v0:
```python
import jax
import jax.numpy as jnp
from jax import lax
from jax.sharding import PartitionSpec as P

ITERS = 2
delta_sq = 0.01
eps = 1e-05


def with_halo(cells, axis, dim):
    count = lax.axis_size(axis)
    ends = count - 1
    head = lax.slice_in_dim(cells, 0, 1, axis=dim)
    tail = lax.slice_in_dim(cells, cells.shape[dim] - 1, cells.shape[dim], axis=dim)
    return jnp.concatenate(
        [
            lax.ppermute(tail, axis, [(i, (i + 1) % count) for i in range(ends)]),
            cells,
            lax.ppermute(head, axis, [((i + 1) % count, i) for i in range(ends)]),
        ],
        axis=dim,
    )


def weiszfeld(values, valid):
    median = jnp.zeros(values.shape[1:], jnp.float32)
    for step in range(ITERS + 1):
        if step == 0:
            weight = valid
        else:
            diff = values - median[None]
            weight = valid / jnp.sqrt(jnp.sum(diff * diff, axis=1) + delta_sq)
        numer = jnp.sum(weight[:, None] * values, axis=0)
        denom = jnp.sum(weight, axis=0)
        median = (numer + median) / (denom + 1.0)
    return median


def body(stack, cloud):
    bands = stack.shape[1]
    rows = stack.shape[2]
    cols = stack.shape[3]
    cloudy = (1 - cloud).astype(jnp.bfloat16)
    rimmed = with_halo(cloudy, "pix", 1).astype(jnp.float32)
    padded = jnp.pad(rimmed, ((0, 0), (0, 0), (1, 1)))
    near = jnp.maximum(padded[:, 1:-1, 1:-1], padded[:, 2:, 1:-1])
    near = jnp.maximum(near, padded[:, :-2, 1:-1])
    near = jnp.maximum(near, padded[:, 1:-1, 2:])
    near = jnp.maximum(near, padded[:, 1:-1, :-2])
    valid = (1.0 - near).astype(jnp.bfloat16)
    planes = jnp.concatenate([stack, valid[:, None]], axis=1)
    planes = lax.all_to_all(planes, "date", 3, 0, tiled=True).astype(jnp.float32)
    median = weiszfeld(planes[:, :bands], planes[:, bands])
    median = lax.all_gather(median, "date", axis=2, tiled=True)
    count = lax.axis_size("pix") * rows * cols
    sums = lax.psum((jnp.sum(median, axis=(1, 2)), jnp.sum(median * median, axis=(1, 2))), "pix")
    mean = sums[0] / count
    var = sums[1] / count - mean * mean
    return (median - mean[:, None, None]) / jnp.sqrt(var[:, None, None] + eps)


def solution(mesh):
    placed = (P("date", None, "pix", None), P("date", "pix", None))
    return jax.shard_map(
        body, mesh=mesh, in_specs=placed, out_specs=P(None, "pix", None), check_vma=False
    )
```

profile of v0, /device:TPU:0, one launch (start us, length us, event | category | flops | bytes accessed | tf_op | source)
XLA Modules:
  0.0 144.7 jit_solution(4334048969689377763)
XLA Ops:
  0.9 2.4 %collective-permute-start = (bf16[1,1,2048]{2,1,0:T(2,128)(2,1)S(1)}, bf16[1,1,2048]{2,1,0:T(2,128)(2,1)S(1)}, u32[]{:S(2)}, u32[]{:S(2)}) collective-permute-start(bf16[1,1,2048]{2,1,0:T(2,128)(2,1)S(1)} %get-tuple-element.11), channel_id=1, source_target_pairs={{0,1},{1,2},{2,3},{4,5},{5,6},{6,7},{8,9},{9,10},{10,11},{12,13},{... | collective-permute-start | bytes 12296 | tf_op jit(solution)/shard_map/ppermute | solution.py:18
  3.3 1.3 collective-permute-start.1
  4.6 3.9 %collective-permute-done.1 = bf16[1,1,2048]{2,1,0:T(2,128)(2,1)S(1)} collective-permute-done((bf16[1,1,2048]{2,1,0:T(2,128)(2,1)S(1)}, bf16[1,1,2048]{2,1,0:T(2,128)(2,1)S(1)}, u32[]{:S(2)}, u32[]{:S(2)}) %collective-permute-start.1) | collective-permute-done | bytes 4128 | tf_op jit(solution)/shard_map/ppermute | solution.py:20
  9.6 4.3 %copy.33 = bf16[1,11,8,2048]{1,2,0,3:T(8,128)(2,1)} copy(bf16[1,11,8,2048]{3,2,1,0:T(8,128)(2,1)S(1)} %pad_maximum_fusion) | data formatting | bytes 720896 | tf_op jit(solution)/shard_map/concatenate | solution.py:52
  14.0 7.3 %reshape.94 = bf16[8,2,11264]{2,1,0:T(2,128)(2,1)S(1)} reshape(bf16[2048,1,8,11]{3,2,1,0:T(8,128)(2,1)} %bitcast.38) | data formatting | bytes 720896
  21.2 16.5 %all_to_all.4 = bf16[8,2,11264]{2,1,0:T(2,128)(2,1)S(1)} all-to-all(bf16[8,2,11264]{2,1,0:T(2,128)(2,1)S(1)} %reshape.94), channel_id=1, replica_groups=mesh['date'=8,'pix'=4] {'date'}, dimensions={0} | all-to-all | bytes 720896 | tf_op jit(solution)/shard_map/all_to_all | solution.py:53
  37.7 10.2 %reshape.95 = bf16[2048,1,8,11]{3,2,1,0:T(8,128)(2,1)} reshape(bf16[8,2,11264]{2,1,0:T(2,128)(2,1)S(1)} %all_to_all.4) | data formatting | bytes 720896
  47.9 17.2 %copy.34 = f32[1,11,8,8,256]{2,4,3,1,0:T(8,128)} copy(bf16[1,11,8,8,256]{1,2,4,3,0:T(8,128)(2,1)} %bitcast.39) | data formatting | bytes 1081344 | tf_op jit(solution)/shard_map/convert_element_type | solution.py:53
  65.1 1.4 fusion.8
  66.5 1.0 reduce_sum.91
  67.6 5.6 %multiply_reduce_fusion.4 = f32[10,8,256]{1,2,0:T(8,128)S(1)} fusion(f32[8,11,8,256]{2,3,0,1:T(8,128)} %bitcast.27, f32[8,8,256]{1,2,0:T(8,128)S(1)} %get-tuple-element.10), kind=kLoop, calls=%fused_computation.4 | loop fusion | flops 307200 | bytes 802816 | tf_op jit(solution)/shard_map/reduce_sum | solution.py:34
  74.0 5.6 %multiply_reduce_fusion.3 = f32[8,8,256]{1,2,0:T(8,128)S(1)} fusion(f32[8,11,8,256]{2,3,0,1:T(8,128)} %bitcast.28, f32[10,8,256]{1,2,0:T(8,128)S(1)} %copy.39), kind=kLoop, calls=%fused_computation.3 | loop fusion | flops 475136 | bytes 802816 | tf_op jit(solution)/shard_map/reduce_sum | solution.py:33
  79.6 1.5 %multiply_reduce_fusion.6 = f32[8,256]{0,1:T(8,128)S(1)} fusion(f32[8,8,256]{1,2,0:T(8,128)S(1)} %multiply_reduce_fusion.3, f32[8,11,8,256]{2,3,0,1:T(8,128)} %bitcast.29), kind=kLoop, calls=%fused_computation.11 | loop fusion | flops 47104 | bytes 139264 | tf_op jit(solution)/shard_map/reduce_sum | solution.py:35
  81.0 1.5 %fusion.1 = f32[8,8,256]{1,2,0:T(8,128)S(1)} fusion(f32[8,8,256]{1,2,0:T(8,128)S(1)} %multiply_reduce_fusion.3, f32[8,11,8,256]{2,3,0,1:T(8,128)} %bitcast.30), kind=kLoop, calls=%fused_computation.8 | loop fusion | flops 32768 | bytes 196608 | tf_op jit(solution)/shard_map/mul | solution.py:34
  82.6 6.6 %multiply_reduce_fusion.2 = f32[10,8,256]{1,2,0:T(8,128)} fusion(f32[8,11,8,256]{2,3,0,1:T(8,128)} %bitcast.31, f32[8,8,256]{1,2,0:T(8,128)S(1)} %fusion.1), kind=kLoop, calls=%fused_computation.2 | loop fusion | flops 307200 | bytes 802816 | tf_op jit(solution)/shard_map/reduce_sum | solution.py:34
  89.2 1.8 %copy.41 = f32[10,8,256]{2,1,0:T(8,128)S(1)} copy(f32[10,8,256]{1,2,0:T(8,128)} %multiply_reduce_fusion.2) | data formatting | bytes 163840 | tf_op jit(solution)/shard_map/reduce_sum | solution.py:34
  91.1 1.5 %copy.43 = f32[10,8,256]{1,2,0:T(8,128)} copy(f32[10,8,256]{2,1,0:T(8,128)S(1)} %add_divide_fusion.1) | data formatting | bytes 163840 | tf_op jit(solution)/shard_map/div | solution.py:36
  92.6 6.1 %multiply_reduce_fusion.1 = f32[8,8,256]{1,2,0:T(8,128)S(1)} fusion(f32[8,11,8,256]{2,3,0,1:T(8,128)} %bitcast.32, f32[10,8,256]{1,2,0:T(8,128)} %copy.43), kind=kLoop, calls=%fused_computation.1 | loop fusion | flops 475136 | bytes 802816 | tf_op jit(solution)/shard_map/reduce_sum | solution.py:33
  98.7 1.5 %multiply_reduce_fusion.5 = f32[8,256]{0,1:T(8,128)S(1)} fusion(f32[8,8,256]{1,2,0:T(8,128)S(1)} %multiply_reduce_fusion.1, f32[8,11,8,256]{2,3,0,1:T(8,128)} %bitcast.33), kind=kLoop, calls=%fused_computation.9 | loop fusion | flops 47104 | bytes 139264 | tf_op jit(solution)/shard_map/reduce_sum | solution.py:35
  100.1 1.5 %fusion = f32[8,8,256]{1,2,0:T(8,128)S(1)} fusion(f32[8,8,256]{1,2,0:T(8,128)S(1)} %multiply_reduce_fusion.1, f32[8,11,8,256]{2,3,0,1:T(8,128)} %bitcast.34), kind=kLoop, calls=%fused_computation.6 | loop fusion | flops 32768 | bytes 196608 | tf_op jit(solution)/shard_map/mul | solution.py:34
  101.6 2.5 %multiply_reduce_fusion = f32[10,8,256]{1,2,0:T(8,128)} fusion(f32[8,11,8,256]{2,3,0,1:T(8,128)S(1)} %bitcast.37, f32[8,8,256]{1,2,0:T(8,128)S(1)} %fusion), kind=kLoop, calls=%fused_computation | loop fusion | flops 307200 | bytes 802816 | tf_op jit(solution)/shard_map/reduce_sum | solution.py:34
  104.1 1.7 %copy.45 = f32[10,8,256]{2,1,0:T(8,128)S(1)} copy(f32[10,8,256]{1,2,0:T(8,128)} %multiply_reduce_fusion) | data formatting | bytes 163840 | tf_op jit(solution)/shard_map/reduce_sum | solution.py:34
  105.9 32.0 %all_gather.3 = f32[10,8,2048]{2,1,0:T(8,128)S(1)} all-gather(f32[10,8,256]{2,1,0:T(8,128)S(1)} %add_divide_fusion), channel_id=1, replica_groups=mesh['date'=8,'pix'=4] {'date'}, dimensions={2}, use_global_device_ids=true | all-gather | bytes 737280 | tf_op jit(solution)/shard_map/all_gather | solution.py:55
  138.1 5.7 %all-reduce.1 = (f32[10]{0:T(128)S(1)}, f32[10]{0:T(128)S(1)}) all-reduce(f32[10]{0:T(128)S(1)} %get-tuple-element.6, f32[10]{0:T(128)S(1)} %get-tuple-element.5), channel_id=1, replica_groups=mesh['date'=8,'pix'=4] {'pix'}, use_global_device_ids=true, to_apply=%region_11.12 | all-reduce | flops 20 | bytes 160 | tf_op jit(solution)/shard_map/psum | solution.py:57
  (27 shorter events, 4.2 us)
Async XLA Ops:
  0.9 3.7 %collective-permute-start = (bf16[1,1,2048]{2,1,0:T(2,128)(2,1)S(1)}, bf16[1,1,2048]{2,1,0:T(2,128)(2,1)S(1)}, u32[]{:S(2)}, u32[]{:S(2)}) collective-permute-start(bf16[1,1,2048]{2,1,0:T(2,128)(2,1)S(1)} %get-tuple-element.11), channel_id=1, source_target_pairs={{0,1},{1,2},{2,3},{4,5},{5,6},{6,7},{8,9},{9,10},{10,11},{12,13},{... | collective-permute-start | bytes 12296 | tf_op jit(solution)/shard_map/ppermute | solution.py:18
  3.3 5.2 %collective-permute-start.1 = (bf16[1,1,2048]{2,1,0:T(2,128)(2,1)S(1)}, bf16[1,1,2048]{2,1,0:T(2,128)(2,1)S(1)}, u32[]{:S(2)}, u32[]{:S(2)}) collective-permute-start(bf16[1,1,2048]{2,1,0:T(2,128)(2,1)S(1)} %get-tuple-element.12), channel_id=1, source_target_pairs={{1,0},{2,1},{3,2},{5,4},{6,5},{7,6},{9,8},{10,9},{11,10},{13,12},{... | collective-permute-start | bytes 12296 | tf_op jit(solution)/shard_map/ppermute | solution.py:20
  89.2 12.4 %slice-start = ((s8[11534336]{0:T(1024)(128)(4,1)}), s8[3145728]{0:T(1024)(128)(4,1)S(1)}, s32[]{:S(2)}) async-start(s8[11534336]{0:T(1024)(128)(4,1)} %bitcast.35), calls=%async_computation.1 | async-start | bytes 6291456
  92.6 9.1 %slice-start.1 = ((s8[11534336]{0:T(1024)(128)(4,1)}), s8[4194304]{0:T(1024)(128)(4,1)S(1)}, s32[]{:S(2)}) async-start(s8[11534336]{0:T(1024)(128)(4,1)} %bitcast.35), calls=%async_computation.2 | async-start | bytes 8388608
  92.6 9.1 %slice-start.2 = ((s8[11534336]{0:T(1024)(128)(4,1)}), s8[4194304]{0:T(1024)(128)(4,1)S(1)}, s32[]{:S(2)}) async-start(s8[11534336]{0:T(1024)(128)(4,1)} %bitcast.35), calls=%async_computation.3 | async-start | bytes 8388608
where the time goes:
time: 145 us
  blocking collectives  54.1 us (37%)
  local copies, waits for them, and re-layouts  46.4 us (32%)
  other arithmetic  36.5 us (25%)
  waiting for transfers between devices  3.88 us (3%)
  starting transfers between devices  3.69 us (3%)
    all_gather x1, blocking collectives, body(): median = lax.all_gather(median, 'date', axis=2, tiled=True)  32 us
    unnamed x8, local copies, waits for them, and re-layouts  17.5 us
    convert_element_type x1, local copies, waits for them, and re-layouts, body(): lax.all_to_all(planes, 'date', 3, 0, tiled=True).astype(jnp.float32)  17.2 us
    all_to_all x1, blocking collectives, body(): lax.all_to_all(planes, 'date', 3, 0, tiled=True).astype(jnp.float32)  16.5 us
    reduce_sum x3, other arithmetic, weiszfeld(): numer = jnp.sum(weight[:, None] * values, axis=0)  14.6 us
    reduce_sum x2, other arithmetic, weiszfeld(): weight = valid / jnp.sqrt(jnp.sum(diff * diff, axis=1) + delta_sq)  11.7 us
    psum x1, blocking collectives, body(): lax.psum((jnp.sum(median, axis=(1, 2)), jnp.sum(median * median, axis=(1,...  5.66 us
    concatenate x1, local copies, waits for them, and re-layouts, body(): planes = jnp.concatenate([stack, valid[:, None]], axis=1)  4.35 us
  transfers between devices with their start and end apart: 2, of which 1 were waited for; matrix products, arithmetic and copies ran while one was open for 0% of the time, Pallas kernels for 0%

commit v1 on v0

--- a/solution.py
+++ b/solution.py
@@ -6,6 +6,18 @@
 ITERS = 2
 delta_sq = 0.01
 eps = 1e-05
+
+
+def get_the_cycles(local_block):
+    return jnp.concatenate(
+        lax.all_to_all(
+            jnp.stack(jnp.split(local_block, lax.axis_size("date"), axis=3)),
+            axis_name="date",
+            split_axis=0,
+            concat_axis=0,
+        ),
+        axis=0,
+    )
 
 
 def with_halo(cells, axis, dim):
@@ -50,7 +62,7 @@
     near = jnp.maximum(near, padded[:, 1:-1, :-2])
     valid = (1.0 - near).astype(jnp.bfloat16)
     planes = jnp.concatenate([stack, valid[:, None]], axis=1)
-    planes = lax.all_to_all(planes, "date", 3, 0, tiled=True).astype(jnp.float32)
+    planes = get_the_cycles(planes).astype(jnp.float32)
     median = weiszfeld(planes[:, :bands], planes[:, bands])
     median = lax.all_gather(median, "date", axis=2, tiled=True)
     count = lax.axis_size("pix") * rows * cols

time: 145 us -> 64.9 us (0.45)
  local copies, waits for them, and re-layouts: 46.4 us -> 0.02 us
  other arithmetic: 36.5 us -> 2.77 us
    unnamed x8 -> x2, local copies, waits for them, and re-layouts: 17.5 us -> 0.01 us
    convert_element_type x1 -> x0, local copies, waits for them, and re-layouts: 17.2 us -> none  [body(): lax.all_to_all(planes, 'date', 3, 0, tiled=True).astype(jnp.float32)]
    reduce_sum x3, other arithmetic: 14.6 us -> 0.16 us  [weiszfeld(): numer = jnp.sum(weight[:, None] * values, axis=0)]
    reduce_sum x2, other arithmetic: 11.7 us -> 0.13 us  [weiszfeld(): weight = valid / jnp.sqrt(jnp.sum(diff * diff, axis=1) + delta_sq)]
    concatenate x1 -> x0, local copies, waits for them, and re-layouts: 4.35 us -> none  [body(): planes = jnp.concatenate([stack, valid[:, None]], axis=1)]
    reduce_sum x3, other arithmetic: 3.94 us -> 0.06 us  [weiszfeld(): denom = jnp.sum(weight, axis=0)]
    reduce_sum x3 -> x0, local copies, waits for them, and re-layouts: 3.86 us -> none  [weiszfeld(): numer = jnp.sum(weight[:, None] * values, axis=0)]
    mul x2, other arithmetic: 2.96 us -> 0.04 us  [weiszfeld(): numer = jnp.sum(weight[:, None] * values, axis=0)]
where the time goes in v1:
time: 64.9 us; the launch traced here: 64.7 us
  blocking collectives  54.1 us (83%)
  waiting for transfers between devices  3.88 us (6%)
  starting transfers between devices  3.69 us (6%)
  other arithmetic  2.77 us (4%)
    all_gather x1, blocking collectives, body(): median = lax.all_gather(median, 'date', axis=2, tiled=True)  32 us
    all_to_all x1, blocking collectives, get_the_cycles(): lax.all_to_all(jnp.stack(jnp.split(local_block, lax.axis_size('date'), ax...  16.5 us
    psum x1, blocking collectives, body(): lax.psum((jnp.sum(median, axis=(1, 2)), jnp.sum(median * median, axis=(1,...  5.66 us
    ppermute x1, waiting for transfers between devices, with_halo(): lax.ppermute(head, axis, [((i + 1) % count, i) for i in range(ends)])  3.88 us
    ppermute x1, starting transfers between devices, with_halo(): lax.ppermute(tail, axis, [(i, (i + 1) % count) for i in range(ends)])  2.4 us
  transfers between devices with their start and end apart: 2, of which 1 were waited for; matrix products, arithmetic and copies ran while one was open for 0% of the time, Pallas kernels for 0%

profile of v1, /device:TPU:0, one launch (start us, length us, event | category | flops | bytes accessed | tf_op | source)
XLA Modules:
  0.0 64.7 jit_solution(7232024814883453630)
XLA Ops:
  0.0 0.0 copy-start
  0.0 0.9 %subtract_convert_fusion = bf16[1,8,2048]{2,1,0:T(8,128)(2,1)S(1)} fusion(s32[1,8,2048]{2,1,0:T(8,128)} %param.3), kind=kLoop, calls=%fused_computation.41 | loop fusion | flops 32768 | bytes 98304 | tf_op jit(solution)/shard_map/convert_element_type | solution.py:56
  0.9 2.4 %collective-permute-start = (bf16[1,1,2048]{2,1,0:T(2,128)(2,1)S(1)}, bf16[1,1,2048]{2,1,0:T(2,128)(2,1)S(1)}, u32[]{:S(2)}, u32[]{:S(2)}) collective-permute-start(bf16[1,1,2048]{2,1,0:T(2,128)(2,1)S(1)} %get-tuple-element.11), channel_id=1, source_target_pairs={{0,1},{1,2},{2,3},{4,5},{5,6},{6,7},{8,9},{9,10},{10,11},{12,13},{... | collective-permute-start | bytes 12296 | tf_op jit(solution)/shard_map/ppermute | solution.py:30
  3.3 1.3 %collective-permute-start.1 = (bf16[1,1,2048]{2,1,0:T(2,128)(2,1)S(1)}, bf16[1,1,2048]{2,1,0:T(2,128)(2,1)S(1)}, u32[]{:S(2)}, u32[]{:S(2)}) collective-permute-start(bf16[1,1,2048]{2,1,0:T(2,128)(2,1)S(1)} %get-tuple-element.12), channel_id=1, source_target_pairs={{1,0},{2,1},{3,2},{5,4},{6,5},{7,6},{9,8},{10,9},{11,10},{13,12},{... | collective-permute-start | bytes 12296 | tf_op jit(solution)/shard_map/ppermute | solution.py:32
  4.6 0.0 collective-permute-done
  4.6 3.9 %collective-permute-done.1 = bf16[1,1,2048]{2,1,0:T(2,128)(2,1)S(1)} collective-permute-done((bf16[1,1,2048]{2,1,0:T(2,128)(2,1)S(1)}, bf16[1,1,2048]{2,1,0:T(2,128)(2,1)S(1)}, u32[]{:S(2)}, u32[]{:S(2)}) %collective-permute-start.1) | collective-permute-done | bytes 4128 | tf_op jit(solution)/shard_map/ppermute | solution.py:32
  8.5 0.1 fusion.15
  8.7 0.0 copy-done
  8.8 16.5 %all_to_all.5 = bf16[8,1,11,8,256]{4,3,2,1,0:T(8,128)(2,1)S(1)} all-to-all(bf16[8,1,11,8,256]{4,3,2,1,0:T(8,128)(2,1)S(1)} %fusion.14), channel_id=1, replica_groups=mesh['date'=8,'pix'=4] {'date'}, dimensions={0} | all-to-all | bytes 720896 | tf_op jit(solution)/shard_map/all_to_all | solution.py:13
  25.3 0.1 bitcast_convert_fusion
  25.3 0.1 multiply_reduce_fusion.5
  25.4 0.1 multiply_reduce_fusion.4
  25.6 0.1 multiply_reduce_fusion.3
  25.6 0.1 multiply_reduce_fusion.2
  25.8 0.1 multiply_reduce_fusion.1
  25.9 32.0 %all_gather.3 = f32[10,8,2048]{2,1,0:T(8,128)S(1)} all-gather(f32[10,8,256]{2,1,0:T(8,128)S(1)} %add_divide_fusion), channel_id=1, replica_groups=mesh['date'=8,'pix'=4] {'date'}, dimensions={2}, use_global_device_ids=true | all-gather | bytes 737280 | tf_op jit(solution)/shard_map/all_gather | solution.py:67
  57.8 0.2 fusion.16
  58.0 5.7 %all-reduce.1 = (f32[10]{0:T(128)S(1)}, f32[10]{0:T(128)S(1)}) all-reduce(f32[10]{0:T(128)S(1)} %get-tuple-element.6, f32[10]{0:T(128)S(1)} %get-tuple-element.5), channel_id=1, replica_groups=mesh['date'=8,'pix'=4] {'pix'}, use_global_device_ids=true, to_apply=%region_11.12 | all-reduce | flops 20 | bytes 160 | tf_op jit(solution)/shard_map/psum | solution.py:69
  63.7 1.0 %subtract_divide_fusion = f32[10,8,2048]{2,1,0:T(8,128)} fusion(f32[10,8,2048]{2,1,0:T(8,128)S(1)} %all_gather.3, f32[10]{0:T(128)S(1)} %get-tuple-element.14, f32[10]{0:T(128)S(1)} %get-tuple-element.13), kind=kLoop, calls=%fused_computation.8 | loop fusion | flops 327680 | bytes 1310800 | tf_op jit(solution)/shard_map/div | solution.py:72
  (22 shorter events, 0.3 us)
Async XLA Ops:
  0.0 8.7 %copy-start = (bf16[1,10,8,2048]{3,2,1,0:T(8,128)(2,1)S(1)}, bf16[1,10,8,2048]{3,2,1,0:T(8,128)(2,1)}, u32[]{:S(2)}) copy-start(bf16[1,10,8,2048]{3,2,1,0:T(8,128)(2,1)} %param.2) | copy-start | bytes 983044
  0.9 3.7 %collective-permute-start = (bf16[1,1,2048]{2,1,0:T(2,128)(2,1)S(1)}, bf16[1,1,2048]{2,1,0:T(2,128)(2,1)S(1)}, u32[]{:S(2)}, u32[]{:S(2)}) collective-permute-start(bf16[1,1,2048]{2,1,0:T(2,128)(2,1)S(1)} %get-tuple-element.11), channel_id=1, source_target_pairs={{0,1},{1,2},{2,3},{4,5},{5,6},{6,7},{8,9},{9,10},{10,11},{12,13},{... | collective-permute-start | bytes 12296 | tf_op jit(solution)/shard_map/ppermute | solution.py:30
  3.3 5.2 %collective-permute-start.1 = (bf16[1,1,2048]{2,1,0:T(2,128)(2,1)S(1)}, bf16[1,1,2048]{2,1,0:T(2,128)(2,1)S(1)}, u32[]{:S(2)}, u32[]{:S(2)}) collective-permute-start(bf16[1,1,2048]{2,1,0:T(2,128)(2,1)S(1)} %get-tuple-element.12), channel_id=1, source_target_pairs={{1,0},{2,1},{3,2},{5,4},{6,5},{7,6},{9,8},{10,9},{11,10},{13,12},{... | collective-permute-start | bytes 12296 | tf_op jit(solution)/shard_map/ppermute | solution.py:32
